TPU v7x, 32 devices: a whole 2x2x4 slice. The times are simulated.
32 devices in a mesh: replica: 2 (over x), data: 4 (over z), table: 4 (over y, core).
Axes of the slice: x: 2, y: 2, z: 4, core: 2. Of those that a mesh axis runs over, the one named last changes fastest.
Arguments:
- tokens: bfloat16 [2048, 768], P(('replica', 'data', 'table')), parts along dimension 0
- grad_out: bfloat16 [2048, 768], P(('replica', 'data', 'table')), parts along dimension 0
- table_u: bfloat16 [131072, 768], P(('replica', 'table')), parts along dimension 0
- table_v: bfloat16 [131072, 768], P(('replica', 'table')), parts along dimension 0
- wanted_ids: int32 [32, 128], P(('replica', 'data', 'table')), parts along dimension 0
- pick_idx: int32 [2048, 4, 32], P(('replica', 'data', 'table')), parts along dimension 0
- gate_val: float32 [2048, 4, 32], P(('replica', 'data', 'table')), parts along dimension 0
Outputs:
- output 1: bfloat16 [2048, 768], P(('replica', 'data', 'table')), parts along dimension 0
- output 2: bfloat16 [2048, 768], P(('replica', 'data', 'table')), parts along dimension 0
- output 3: bfloat16 [131072, 768], P(('replica', 'table')), parts along dimension 0
- output 4: bfloat16 [131072, 768], P(('replica', 'table')), parts along dimension 0
There are 2 independent parts. A program takes and returns all parts, laid end to end along the dimension named above; each array names one.
All inputs are finite; a program needn't handle non-finite values.
Results may differ from a plain program's by a relative error of at most 0.00789345.
Values are sent between devices in bfloat16 or wider.
A program may use at most 1 GiB of HBM per device.

v0:
```python
import math
import jax
import jax.numpy as jnp
from jax import lax
from jax.sharding import PartitionSpec as P, NamedSharding


def gelu_pair(pre_act):
    cdf_val = 0.5 * (1.0 + lax.erf(pre_act * 0.7071067811865476))
    pdf_val = jnp.exp(-0.5 * pre_act * pre_act) * 0.3989422804014327
    return pre_act * cdf_val, cdf_val + pre_act * pdf_val


def token_pass(tok_loc, dy_loc, rows_u, rows_v, pick_loc, gate_loc):
    tok_local, width = tok_loc.shape
    sel_tok = pick_loc.shape[1] * pick_loc.shape[2]
    block_len = math.gcd(tok_local, max(1, 8192 // sel_tok))
    num_blocks = tok_local // block_len
    inputs = (tok_loc.reshape(num_blocks, block_len, width), dy_loc.reshape(num_blocks, block_len, width), pick_loc.reshape(num_blocks, block_len, sel_tok), gate_loc.reshape(num_blocks, block_len, sel_tok))

    def body(acc_pair, block_in):
        acc_u, acc_v = acc_pair
        x_blk, dy_blk, pick_blk, gate_blk = block_in
        sel_u = jnp.take(rows_u, pick_blk, axis=0, mode='clip')
        sel_v = jnp.take(rows_v, pick_blk, axis=0, mode='clip')
        pre_act = jnp.einsum('bsd,bd->bs', sel_u, x_blk, preferred_element_type=jnp.float32)
        act_val, slope_val = gelu_pair(pre_act)
        weight = gate_blk * act_val
        y_blk = jnp.einsum('bs,bsd->bd', weight, sel_v, preferred_element_type=jnp.float32)
        v_dot_dy = jnp.einsum('bsd,bd->bs', sel_v, dy_blk, preferred_element_type=jnp.float32)
        coef_sel = gate_blk * slope_val * v_dot_dy
        dx_blk = jnp.einsum('bs,bsd->bd', coef_sel, sel_u, preferred_element_type=jnp.float32)
        flat_pick = pick_blk.reshape(-1)
        acc_u = acc_u.at[flat_pick].add((coef_sel[:, :, None] * x_blk[:, None, :]).reshape(-1, width))
        acc_v = acc_v.at[flat_pick].add((weight[:, :, None] * dy_blk[:, None, :]).reshape(-1, width))
        return (acc_u, acc_v), (y_blk.astype(jnp.bfloat16), dx_blk.astype(jnp.bfloat16))

    zero_acc = jnp.zeros((rows_u.shape[0], width), jnp.float32)
    (acc_u, acc_v), (y_st, dx_st) = lax.scan(body, (zero_acc, zero_acc), inputs)
    return y_st.reshape(tok_local, width), dx_st.reshape(tok_local, width), acc_u, acc_v


def solution(mesh):
    table_n = mesh.shape['table']
    tok_spec = P(('replica', 'data', 'table'))
    row_spec = P(('replica', 'table'))

    def device_step(tok_loc, dy_loc, u_loc, v_loc, wanted_loc, pick_loc, gate_loc):
        n_local, width = u_loc.shape
        pool_len = wanted_loc.shape[1] // table_n
        owner_base = jnp.arange(table_n, dtype=jnp.int32)[:, None] * n_local
        requests = wanted_loc.reshape(table_n, pool_len) - owner_base
        asked_rows = lax.all_to_all(requests, 'table', 0, 0, tiled=True)
        sent_u = jnp.take(u_loc, asked_rows, axis=0, mode='clip')
        sent_v = jnp.take(v_loc, asked_rows, axis=0, mode='clip')
        rows_u = lax.all_to_all(sent_u, 'table', 0, 0, tiled=True).reshape(table_n * pool_len, width)
        rows_v = lax.all_to_all(sent_v, 'table', 0, 0, tiled=True).reshape(table_n * pool_len, width)
        y_loc, dx_loc, part_u, part_v = token_pass(tok_loc, dy_loc, rows_u, rows_v, pick_loc, gate_loc)
        back_u = lax.all_to_all(part_u.astype(jnp.bfloat16).reshape(table_n, pool_len, width), 'table', 0, 0, tiled=True)
        back_v = lax.all_to_all(part_v.astype(jnp.bfloat16).reshape(table_n, pool_len, width), 'table', 0, 0, tiled=True)
        flat_rows = asked_rows.reshape(-1)
        grad_u = jnp.zeros((n_local, width), jnp.float32).at[flat_rows].add(back_u.reshape(-1, width).astype(jnp.float32))
        grad_v = jnp.zeros((n_local, width), jnp.float32).at[flat_rows].add(back_v.reshape(-1, width).astype(jnp.float32))
        grad_u = lax.psum(grad_u, 'data')
        grad_v = lax.psum(grad_v, 'data')
        return y_loc, dx_loc, grad_u.astype(jnp.bfloat16), grad_v.astype(jnp.bfloat16)

    return jax.shard_map(device_step, mesh=mesh, in_specs=(tok_spec, tok_spec, row_spec, row_spec, tok_spec, tok_spec, tok_spec), out_specs=(tok_spec, tok_spec, row_spec, row_spec), check_vma=False)
```

profile of v0, /device:TPU:0, one launch (start us, length us, event | category | flops | bytes accessed | tf_op | source)
XLA Modules:
  0.0 3628.1 jit_solution(17076993174621837954)
XLA Ops:
  1.2 1.3 reduce.8
  3.2 4.3 all-to-all-start
  7.5 0.9 copy.19
  9.7 0.9 convert_element_type.49
  11.9 13.0 gather_fusion.2
  25.0 13.0 gather_fusion
  38.0 3.4 all-to-all-start.1
  41.4 5.0 all-to-all-done.1
  46.4 3.5 all-to-all-start.2
  50.0 34.4 gather_fusion.1
  84.5 7.9 fusion.8
  92.5 34.4 gather_fusion.3
  127.0 7.9 fusion.6
  135.1 6.3 fusion.25
  141.6 10.6 bitcast_multiply_fusion.1
  152.2 53.7 %scatter_custom_fusion = f32[128,768]{1,0:T(8,128)S(1)} fusion(s32[8192]{0:T(1024)S(1)} %bitcast.72, f32[8192,768]{1,0:T(8,128)} %bitcast_multiply_fusion.1, f32[]{:T(128)} %constant.40.clone.1), kind=kCustom, calls=%fused_computation.24 | custom fusion | flops 6291456 | bytes 393728 | tf_op jit(solution)/shard_map/while/body/eval_jaxpr/scatter-add | solution.py:34
  206.6 3.6 all-to-all-start.3
  210.2 6.3 fusion.26
  216.6 10.6 bitcast_multiply_fusion
  227.2 53.7 %scatter_custom_fusion.2 = f32[128,768]{1,0:T(8,128)S(1)} fusion(s32[8192]{0:T(1024)S(1)} %bitcast.73, f32[8192,768]{1,0:T(8,128)} %bitcast_multiply_fusion, f32[]{:T(128)} %constant.40.clone.1), kind=kCustom, calls=%fused_computation.22 | custom fusion | flops 6291456 | bytes 393728 | tf_op jit(solution)/shard_map/while/body/eval_jaxpr/scatter-add | solution.py:35
  281.6 3.4 all-to-all-start.4
  285.7 21.4 scatter_custom_fusion.1
  307.1 21.2 scatter_custom_fusion.3
  328.3 3299.4 %all-reduce.2 = (bf16[16384,768]{1,0:T(8,128)(2,1)}, bf16[16384,768]{1,0:T(8,128)(2,1)}) all-reduce(f32[16384,768]{1,0:T(8,128)} %scatter_custom_fusion.1, f32[16384,768]{1,0:T(8,128)} %scatter_custom_fusion.3), channel_id=1, replica_groups=mesh['replica'=2,'data'=4,'table'=4] {'data'}, use_global_device_ids=true, to_apply=%region_2.3 | all-reduce | flops 25165824 | bytes 150994944 | tf_op jit(solution)/shard_map/psum | solution.py:64
  (34 shorter events, 6.5 us)
Async XLA Ops:
  3.2 7.9 all-to-all-start
  38.0 8.4 all-to-all-start.1
  46.4 46.0 %all-to-all-start.2 = ((bf16[4,32,768]{2,1,0:T(8,128)(2,1)}), bf16[4,32,768]{2,1,0:T(8,128)(2,1)S(1)}, u32[]{:S(2)}, u32[]{:S(2)}) async-start(bf16[4,32,768]{2,1,0:T(8,128)(2,1)} %bitcast.8), calls=%async_computation.2 | async-start | bytes 393216 | tf_op jit(solution)/shard_map/all_to_all | solution.py:57
  50.0 34.5 copy-start
  92.5 34.5 copy-start.1
  92.5 42.5 %copy-start.2 = (f32[64,4,32]{0,2,1:T(8,128)S(1)}, f32[64,4,32]{0,2,1:T(8,128)}, u32[]{:S(2)}) copy-start(f32[64,4,32]{0,2,1:T(8,128)} %param.13) | copy-start | bytes 98308
  206.6 75.0 %all-to-all-start.3 = ((bf16[4,32,768]{2,1,0:T(8,128)(2,1)}), bf16[4,32,768]{2,1,0:T(8,128)(2,1)S(1)}, u32[]{:S(2)}, u32[]{:S(2)}) async-start(bf16[4,32,768]{2,1,0:T(8,128)(2,1)} %bitcast.20), calls=%async_computation.3 | async-start | bytes 393216 | tf_op jit(solution)/shard_map/all_to_all | solution.py:59
  281.6 25.5 all-to-all-start.4
where the time goes:
time: 3640 us; the launch traced here: 3630 us
  blocking collectives  3300 us (91%)
  other arithmetic  177 us (5%)
  local copies, waits for them, and re-layouts  98.2 us (3%)
    psum x1, blocking collectives, device_step(): grad_u = lax.psum(grad_u, 'data')  3300 us
  transfers between devices with their start and end apart: 5, of which 2 were waited for; matrix products, arithmetic and copies ran while one was open for 4% of the time, Pallas kernels for 0%

commit v1 on v0

v1 whole, which is shorter than its diff:
```python
import functools

import jax
import jax.numpy as jnp
from jax import lax
from jax.experimental import pallas as pl
from jax.experimental.pallas import tpu as pltpu
from jax.sharding import PartitionSpec as P

MESH = pl.DeviceIdType.MESH
F32 = jnp.float32
BF16 = jnp.bfloat16
VMEM = pl.BlockSpec(memory_space=pltpu.VMEM)
ANY = pl.BlockSpec(memory_space=pl.ANY)
NT = (((1,), (1,)), ((), ()))
TN = (((0,), (0,)), ((), ()))
BIG = 60 * 1024 * 1024


def gelu_pair(pre_act):
    cdf_val = 0.5 * (1.0 + lax.erf(pre_act * 0.7071067811865476))
    pdf_val = jnp.exp(-0.5 * pre_act * pre_act) * 0.3989422804014327
    return pre_act * cdf_val, cdf_val + pre_act * pdf_val


def split3(val):
    one = val.astype(BF16)
    rest = val - one.astype(F32)
    two = rest.astype(BF16)
    three = (rest - two.astype(F32)).astype(BF16)
    return one, two, three


def dot(a, b, dims=None):
    if dims is None:
        return jnp.dot(a, b, preferred_element_type=F32)
    return lax.dot_general(a, b, dims, preferred_element_type=F32)


def gate_kernel(pick_ref, gate_ref, ids_ref, out_ref):
    sel, tok = pick_ref.shape
    half = sel // 2
    row = lax.broadcasted_iota(jnp.int32, (half, 2 * tok), 0)

    def body(i, acc):
        base = pl.multiple_of(i * 8, 8)
        pick = pick_ref[pl.ds(base, 8), :]
        gate = gate_ref[pl.ds(base, 8), :]
        pick = jnp.concatenate([pick, pick - half], axis=1)
        gate = jnp.concatenate([gate, gate], axis=1)
        for j in range(8):
            acc = acc + jnp.where(row == pick[j : j + 1, :], gate[j : j + 1, :], 0.0)
        return acc

    out_ref[0:half, :] = lax.fori_loop(0, sel // 8, body, jnp.zeros((half, 2 * tok), F32))
    out_ref[half : half + 8, :] = jnp.broadcast_to(ids_ref[...].astype(F32), (8, sel))


def share_kernel(x_ref, dy_ref, g_ref, tx, ty, gx, ssem, rsem):
    z = lax.axis_index("data")
    t = lax.axis_index("table")
    last = 3
    y, c = t // 2, lax.rem(t, 2)
    y_peer = {"table": (1 - y) * 2 + c}
    c_peer = {"table": y * 2 + (1 - c)}
    up, down = {"data": z + 1}, {"data": z - 1}
    me = z * 4 + t
    tok = x_ref.shape[0]

    bar = pltpu.get_barrier_semaphore()
    for peer in (y_peer, c_peer):
        pl.semaphore_signal(bar, inc=1, device_id=peer, device_id_type=MESH)

    @pl.when(z < last)
    def _():
        pl.semaphore_signal(bar, inc=1, device_id=up, device_id_type=MESH)

    @pl.when(z > 0)
    def _():
        pl.semaphore_signal(bar, inc=1, device_id=down, device_id_type=MESH)

    pl.semaphore_wait(bar, 2 + (z < last).astype(jnp.int32) + (z > 0).astype(jnp.int32))

    own = (g_ref, x_ref, dy_ref)
    outs = (gx, tx, ty)

    def place(k, slot):
        if k == 0:
            return gx.at[slot]
        return outs[k].at[pl.ds(pl.multiple_of(slot * tok, tok), tok), :]

    def copy(k, slot, lane, peer, src=None):
        ref = place(k, slot)
        return pltpu.make_async_remote_copy(
            src_ref=ref if src is None else src, dst_ref=ref,
            send_sem=ssem.at[k, lane, slot], recv_sem=rsem.at[k, slot],
            device_id=peer, device_id_type=MESH,
        )

    UP, DOWN, YY, CC = range(4)
    for k in range(3):
        @pl.when(z < last)
        def _():
            copy(k, me, UP, up, own[k]).start()

        @pl.when(z > 0)
        def _():
            copy(k, me, DOWN, down, own[k]).start()

        copy(k, me, YY, y_peer, own[k]).start()
        copy(k, me, CC, c_peer, own[k]).start()

    gx[me] = g_ref[...]
    tx[pl.ds(pl.multiple_of(me * tok, tok), tok), :] = x_ref[...]
    ty[pl.ds(pl.multiple_of(me * tok, tok), tok), :] = dy_ref[...]

    t_y = (1 - y) * 2 + c
    t_c = y * 2 + (1 - c)
    t_yc = (1 - y) * 2 + (1 - c)

    def from_y(slot):
        for k in range(3):
            copy(k, slot, CC, c_peer).wait_recv()
            copy(k, slot, CC, c_peer).start()

    def level(d):
        for k in range(3):
            @pl.when(z - d >= 0)
            def _():
                slot = (z - d) * 4 + t
                copy(k, slot, UP, up).wait_recv()

                @pl.when(z < last)
                def _():
                    copy(k, slot, UP, up).start()

                copy(k, slot, YY, y_peer).start()
                copy(k, slot, CC, c_peer).start()

            @pl.when(z + d <= last)
            def _():
                slot = (z + d) * 4 + t
                copy(k, slot, DOWN, down).wait_recv()

                @pl.when(z > 0)
                def _():
                    copy(k, slot, DOWN, down).start()

                copy(k, slot, YY, y_peer).start()
                copy(k, slot, CC, c_peer).start()

    def y_level(d):
        @pl.when(z - d >= 0)
        def _():
            from_y((z - d) * 4 + t_y)

        @pl.when(z + d <= last)
        def _():
            from_y((z + d) * 4 + t_y)

    level(1)
    from_y(z * 4 + t_y)
    level(2)
    y_level(1)
    level(3)
    y_level(2)
    y_level(3)

    for zz in range(4):
        for tt in (t_c, t_yc):
            for k in range(3):
                copy(k, zz * 4 + tt, CC, c_peer).wait_recv()

    for zz in range(4):
        for k in range(3):
            slot = zz * 4 + t
            copy(k, slot, YY, y_peer).wait_send()
            copy(k, slot, CC, c_peer).wait_send()
            copy(k, zz * 4 + t_y, CC, c_peer).wait_send()

            @pl.when((zz <= z) & (z < last))
            def _():
                copy(k, slot, UP, up).wait_send()

            @pl.when((zz >= z) & (z > 0))
            def _():
                copy(k, slot, DOWN, down).wait_send()


def grad_kernel(u_hbm, v_hbm, tx, ty, gx, du_hbm, dv_hbm, ru_out, rv_out,
                zbuf, ugrp, vgrp, uacc, vacc, rows_u, rows_v, pu, pv, vslot, sslot,
                zsem, gsem, ssem, psem):
    z = lax.axis_index("data")
    r = lax.axis_index("table")
    n_local, width = u_hbm.shape
    n_ent = rows_u.shape[0]
    zrows = zbuf.shape[0]
    zbuf[...] = jnp.zeros_like(zbuf)

    ids = jnp.concatenate([gx[e, 64:65, :] for e in range(16)], axis=0)
    pick = ids[:, 0:32]
    for o in range(1, 4):
        pick = jnp.where(r == o, ids[:, o * 32 : o * 32 + 32], pick)
    pick = pick - (r * n_local).astype(F32)
    idrow = jnp.concatenate([pick[e : e + 1, :] for e in range(16)], axis=1)
    ii = lax.broadcasted_iota(jnp.int32, (n_ent, n_ent), 0)
    jj = lax.broadcasted_iota(jnp.int32, (n_ent, n_ent), 1)

    def lanes(cond, val):
        return jnp.sum(jnp.where(cond, val, 0.0), axis=1, keepdims=True)

    def subl(cond, val):
        return jnp.sum(jnp.where(cond, val, 0.0), axis=0, keepdims=True)

    idcol = lanes(ii == jj, jnp.broadcast_to(idrow, (n_ent, n_ent)))
    grow, gcol = jnp.floor(idrow * 0.125), jnp.floor(idcol * 0.125)
    same = gcol == grow
    lead_col = jnp.where(lanes(same & (jj < ii), 1.0) == 0.0, 1.0, 0.0)
    lead_row = jnp.where(subl(same & (ii < jj), 1.0) == 0.0, 1.0, 0.0)
    rank_col = lanes(jj < ii, jnp.broadcast_to(lead_row, (n_ent, n_ent)))
    rank_row = subl(ii < jj, jnp.broadcast_to(lead_col, (n_ent, n_ent)))
    hit_c = (rank_col.astype(jnp.int32) == jj) & (lead_col > 0.0)
    hit_r = (rank_row.astype(jnp.int32) == ii) & (lead_row > 0.0)
    count = jnp.sum(lead_row, axis=1, keepdims=True)
    slot_row = subl(hit_c, jnp.broadcast_to(gcol, (n_ent, n_ent)))
    slot_col = lanes(hit_r, jnp.broadcast_to(grow, (n_ent, n_ent)))
    lane_id = lax.broadcasted_iota(jnp.int32, (1, n_ent), 1)
    sub_id = lax.broadcasted_iota(jnp.int32, (n_ent, 1), 0)
    icount = count.astype(jnp.int32)
    vslot[0:1, :] = slot_row.astype(jnp.int32)
    vslot[1:2, :] = jnp.broadcast_to(icount, (1, n_ent))
    slot_row = jnp.where(lane_id < icount, slot_row, -1.0)
    slot_col = jnp.where(sub_id < icount, slot_col, -1.0)

    def fill(i, table, k):
        return pltpu.make_async_copy(zbuf, table.at[pl.ds(i * zrows, zrows), :], zsem.at[k])

    for i in range(n_local // zrows):
        fill(i, du_hbm, 0).start()
        fill(i, dv_hbm, 1).start()
    to_smem = pltpu.make_async_copy(vslot, sslot, ssem)
    to_smem.start()
    to_smem.wait()
    n_slot = sslot[1, 0]
    n_blk = (n_slot + 31) // 32

    def fetch(k, table, grp, s):
        g = pl.multiple_of(sslot[0, k] * 8, 8)
        return pltpu.make_async_copy(table.at[pl.ds(g, 8), :], grp.at[pl.ds(pl.multiple_of(k * 8, 8), 8), :], gsem.at[s])

    def start_fetch(k, carry):
        fetch(k, u_hbm, ugrp, 0).start()
        fetch(k, v_hbm, vgrp, 1).start()
        return carry

    def wait_fetch(k, carry):
        fetch(k, u_hbm, ugrp, 0).wait()
        fetch(k, v_hbm, vgrp, 1).wait()
        return carry

    lax.fori_loop(0, n_blk * 32, start_fetch, 0)
    lax.fori_loop(0, n_blk * 32, wait_fetch, 0)

    qrow = lax.broadcasted_iota(jnp.int32, (1, 256), 1)
    qcol = lax.broadcasted_iota(jnp.int32, (256, 1), 0)
    uacc[...] = jnp.zeros_like(uacc)
    vacc[...] = jnp.zeros_like(vacc)
    kk = lax.broadcasted_iota(jnp.int32, (n_ent, 256), 0)
    qk = lax.broadcasted_iota(jnp.int32, (n_ent, 256), 1) >> 3

    def take_rows(b, carry):
        rowid = 8.0 * subl(kk == qk + b * 32, jnp.broadcast_to(slot_col, (n_ent, 256))) + (qrow & 7).astype(F32)
        pickm = jnp.where(idcol == rowid, 1.0, 0.0).astype(BF16)
        base = pl.multiple_of(b * 256, 256)
        uacc[...] += dot(pickm, ugrp[pl.ds(base, 256), :])
        vacc[...] += dot(pickm, vgrp[pl.ds(base, 256), :])
        return carry

    lax.fori_loop(0, n_blk, take_rows, 0)
    rows_u[...] = uacc[...].astype(BF16)
    rows_v[...] = vacc[...].astype(BF16)
    mine = pl.ds(pl.multiple_of(z * 128, 128), 128)
    ru_out[...] = rows_u[mine, :]
    rv_out[...] = rows_v[mine, :]

    diag = (lax.broadcasted_iota(jnp.int32, (128, 256), 0) >> 5) == (lax.broadcasted_iota(jnp.int32, (128, 256), 1) >> 6)
    for d in range(4):
        x4, dy4 = tx[256 * d : 256 * d + 256, :], ty[256 * d : 256 * d + 256, :]
        u4, v4 = rows_u[128 * d : 128 * d + 128, :], rows_v[128 * d : 128 * d + 128, :]
        gates = []
        for e in range(4 * d, 4 * d + 4):
            part = gx[e, pl.ds(pl.multiple_of(lax.rem(r, 2) * 32, 32), 32), :]
            part = jnp.where(r >= 2, part[:, 64:128], part[:, 0:64])
            gates.append(jnp.concatenate([part] * 4, axis=1))
        g4 = jnp.concatenate(gates, axis=0)
        act, slope = gelu_pair(dot(u4, x4, NT))
        b4 = dot(v4, dy4, NT)
        w4 = jnp.where(diag, g4 * act, 0.0)
        c4 = jnp.where(diag, g4 * slope * b4, 0.0)
        for coef, val, out in ((c4, x4, pu), (w4, dy4, pv)):
            full = dot(jnp.concatenate(split3(coef), axis=0), val)
            full = full[0:128] + full[128:256] + full[256:384]
            for k, term in enumerate(split3(full)):
                out[k, 128 * d : 128 * d + 128, :] = term

    kq = lax.broadcasted_iota(jnp.int32, (256, n_ent), 1)
    qq = lax.broadcasted_iota(jnp.int32, (256, n_ent), 0) >> 3

    def put_rows(b, carry):
        rowid = 8.0 * lanes(kq == qq + b * 32, jnp.broadcast_to(slot_row, (256, n_ent))) + (qcol & 7).astype(F32)
        spread = jnp.where(rowid == idrow, 1.0, 0.0).astype(BF16)
        base = pl.multiple_of(b * 256, 256)
        ugrp[pl.ds(base, 256), :] = (dot(spread, pu[0]) + dot(spread, pu[1]) + dot(spread, pu[2])).astype(BF16)
        vgrp[pl.ds(base, 256), :] = (dot(spread, pv[0]) + dot(spread, pv[1]) + dot(spread, pv[2])).astype(BF16)
        return carry

    lax.fori_loop(0, n_blk, put_rows, 0)
    for i in range(n_local // zrows):
        fill(i, du_hbm, 0).wait()
        fill(i, dv_hbm, 1).wait()

    def patch(k, table, grp, s):
        g = pl.multiple_of(sslot[0, k] * 8, 8)
        return pltpu.make_async_copy(grp.at[pl.ds(pl.multiple_of(k * 8, 8), 8), :], table.at[pl.ds(g, 8), :], psem.at[s])

    def start_patch(k, carry):
        patch(k, du_hbm, ugrp, 0).start()
        patch(k, dv_hbm, vgrp, 1).start()
        return carry

    def wait_patch(k, carry):
        patch(k, du_hbm, ugrp, 0).wait()
        patch(k, dv_hbm, vgrp, 1).wait()
        return carry

    lax.fori_loop(0, n_slot, start_patch, 0)
    lax.fori_loop(0, n_slot, wait_patch, 0)


def token_kernel(ru, rv, x_ref, dy_ref, g_ref, y_out, dx_out, ubuf, vbuf, ssem, rsem):
    r = lax.axis_index("table")
    bar = pltpu.get_barrier_semaphore()
    for s in range(1, 4):
        pl.semaphore_signal(bar, inc=1, device_id={"table": lax.rem(r + s, 4)}, device_id_type=MESH)
    pl.semaphore_wait(bar, 3)
    mine = pl.ds(pl.multiple_of(r * 32, 32), 32)

    def send(k, s):
        to = lax.rem(r + s, 4)
        return pltpu.make_async_remote_copy(
            src_ref=(ru, rv)[k].at[pl.ds(pl.multiple_of(to * 32, 32), 32), :],
            dst_ref=(ubuf, vbuf)[k].at[mine, :],
            send_sem=ssem.at[k, s], recv_sem=rsem.at[k, s],
            device_id={"table": to}, device_id_type=MESH,
        )

    for k in range(2):
        for s in (2, 1, 3):
            send(k, s).start()
    ubuf[mine, :] = ru[mine, :]
    vbuf[mine, :] = rv[mine, :]
    gates = jnp.concatenate([g_ref[0:64, 0:64], g_ref[0:64, 64:128]], axis=0)
    for s in range(1, 4):
        send(0, s).wait_recv()
    act, slope = gelu_pair(dot(ubuf[...], x_ref[...], NT))
    for s in range(1, 4):
        send(1, s).wait_recv()
    b_val = dot(vbuf[...], dy_ref[...], NT)
    w_val = jnp.transpose(gates * act)
    c_val = jnp.transpose(gates * slope * b_val)
    for coef, rows, out in ((w_val, vbuf, y_out), (c_val, ubuf, dx_out)):
        full = dot(jnp.concatenate(split3(coef), axis=0), rows[...])
        out[...] = (full[0:64] + full[64:128] + full[128:192]).astype(BF16)
    for k in range(2):
        for s in range(1, 4):
            send(k, s).wait_send()


def solution(mesh):
    tok_spec = P(('replica', 'data', 'table'))
    row_spec = P(('replica', 'table'))

    def device_step(tok, dy, u, v, wanted, pick, gate):
        n_tok, width = tok.shape
        n_local = u.shape[0]
        sel = pick.shape[1] * pick.shape[2]
        pick_t = jnp.transpose(pick, (1, 2, 0)).reshape(sel, n_tok)
        gate_t = jnp.transpose(gate, (1, 2, 0)).reshape(sel, n_tok)
        shape = jax.ShapeDtypeStruct
        g_own = pl.pallas_call(
            gate_kernel, out_shape=shape((72, 128), F32), in_specs=[VMEM] * 3, out_specs=VMEM,
        )(pick_t, gate_t, wanted)
        tx, ty, gx = pl.pallas_call(
            share_kernel,
            out_shape=[shape((16 * n_tok, width), BF16)] * 2 + [shape((16, 72, 128), F32)],
            in_specs=[VMEM] * 3, out_specs=[VMEM] * 3,
            scratch_shapes=[pltpu.SemaphoreType.DMA((3, 4, 16)), pltpu.SemaphoreType.DMA((3, 16))],
            compiler_params=pltpu.CompilerParams(collective_id=0, has_side_effects=True),
        )(tok, dy, g_own)
        du, dv, ru, rv = pl.pallas_call(
            grad_kernel,
            out_shape=[shape((n_local, width), BF16)] * 2 + [shape((128, width), BF16)] * 2,
            in_specs=[ANY, ANY, VMEM, VMEM, VMEM], out_specs=[ANY, ANY, VMEM, VMEM],
            scratch_shapes=[
                pltpu.VMEM((512, width), BF16), pltpu.VMEM((4096, width), BF16), pltpu.VMEM((4096, width), BF16),
                pltpu.VMEM((512, width), F32), pltpu.VMEM((512, width), F32),
                pltpu.VMEM((512, width), BF16), pltpu.VMEM((512, width), BF16),
                pltpu.VMEM((3, 512, width), BF16), pltpu.VMEM((3, 512, width), BF16),
                pltpu.VMEM((8, 512), jnp.int32), pltpu.SMEM((8, 512), jnp.int32),
                pltpu.SemaphoreType.DMA((2,)), pltpu.SemaphoreType.DMA((2,)),
                pltpu.SemaphoreType.DMA, pltpu.SemaphoreType.DMA((2,)),
            ],
            compiler_params=pltpu.CompilerParams(vmem_limit_bytes=BIG),
        )(u, v, tx, ty, gx)
        y, dx = pl.pallas_call(
            token_kernel,
            out_shape=[shape((n_tok, width), BF16)] * 2,
            in_specs=[VMEM] * 5, out_specs=[VMEM] * 2,
            scratch_shapes=[
                pltpu.VMEM((128, width), BF16), pltpu.VMEM((128, width), BF16),
                pltpu.SemaphoreType.DMA((2, 4)), pltpu.SemaphoreType.DMA((2, 4)),
            ],
            compiler_params=pltpu.CompilerParams(collective_id=1, has_side_effects=True),
        )(ru, rv, tok, dy, g_own)
        return y, dx, du, dv

    return jax.shard_map(device_step, mesh=mesh, in_specs=(tok_spec, tok_spec, row_spec, row_spec, tok_spec, tok_spec, tok_spec), out_specs=(tok_spec, tok_spec, row_spec, row_spec), check_vma=False)
```

time: 3640 us -> 69.1 us (0.02)
  blocking collectives: 3300 us -> 0 us
  other arithmetic: 177 us -> 0 us
  local copies, waits for them, and re-layouts: 98.2 us -> 3.08 us
  Pallas kernels: 0 us -> 64.8 us
    psum x1 -> x0, blocking collectives: 3300 us -> none  [device_step(): grad_u = lax.psum(grad_u, 'data')]
    scatter-add x4 -> x0, other arithmetic: 150 us -> none  [the longest x1 53.7 us: body(): acc_u.at[flat_pick]]
    gather x4 -> x0, local copies, waits for them, and re-layouts: 95 us -> none  [the longest x1 34.4 us: body(): sel_u = jnp.take(rows_u, pick_blk, axis=0, mode='clip')]
    pallas_call x0 -> x4, Pallas kernels: none -> 64.8 us  [the longest x1 30.9 us: device_step(): pl.pallas_call(share_kernel, out_shape=[shape((16 * n_tok, width), BF16)]...]
  transfers between devices with their start and end apart: 5 -> 0, of which waited for: 2 -> 0; matrix products, arithmetic and copies ran while one was open for 4% -> 0% of each run, Pallas kernels for 0% -> 0%
where the time goes in v1:
time: 69.1 us; the launch traced here: 68.6 us
  Pallas kernels  64.8 us (94%)
  local copies, waits for them, and re-layouts  3.08 us (4%)
    pallas_call x1, Pallas kernels, device_step(): pl.pallas_call(share_kernel, out_shape=[shape((16 * n_tok, width), BF16)]...  30.9 us
    pallas_call x1, Pallas kernels, device_step(): pl.pallas_call(grad_kernel, out_shape=[shape((n_local, width), BF16)] * 2...  21.6 us
    pallas_call x1, Pallas kernels, device_step(): pl.pallas_call(token_kernel, out_shape=[shape((n_tok, width), BF16)] * 2,...  9.23 us
    pallas_call x1, Pallas kernels, device_step(): pl.pallas_call(gate_kernel, out_shape=shape((72, 128), F32), in_specs=[VM...  3.17 us
    unnamed x2, local copies, waits for them, and re-layouts  3.08 us

profile of v1, /device:TPU:0, one launch (start us, length us, event | category | flops | bytes accessed | tf_op | source)
XLA Modules:
  0.0 68.6 jit_solution(17789136066712371708)
XLA Ops:
  0.6 3.2 %shard_map.102.g_ref = f32[72,128]{1,0:T(8,128)} custom-call(s32[128,64]{1,0:T(8,128)} %bitcast.6, f32[128,64]{1,0:T(8,128)} %bitcast.7, s32[1,128]{1,0:T(1,128)} %ids_ref.1), custom_call_target="tpu_custom_call" | custom-call | tf_op jit(solution)/shard_map/pallas_call | solution.py:390
  3.8 30.9 %shard_map.103 = (bf16[1024,768]{1,0:T(8,128)(2,1)}, bf16[1024,768]{1,0:T(8,128)(2,1)}, f32[16,72,128]{2,1,0:T(8,128)}) custom-call(bf16[64,768]{1,0:T(8,128)(2,1)} %x_ref.3, bf16[64,768]{1,0:T(8,128)(2,1)} %dy_ref.3, f32[72,128]{1,0:T(8,128)} %shard_map.102.g_ref), custom_call_target="tpu_custom_call" | custom-call | tf_op jit(solution)/shard_map/pallas_call | solution.py:393
  34.7 21.6 %shard_map.104 = (bf16[16384,768]{1,0:T(8,128)(2,1)}, bf16[16384,768]{1,0:T(8,128)(2,1)}, bf16[128,768]{1,0:T(8,128)(2,1)}, bf16[128,768]{1,0:T(8,128)(2,1)}) custom-call(bf16[16384,768]{1,0:T(8,128)(2,1)} %u_hbm.1, bf16[16384,768]{1,0:T(8,128)(2,1)} %v_hbm.1, bf16[1024,768]{1,0:T(8,128)(2,1)} %get-tuple-element.13.tx, ...), custom_call_target="tpu_custom_call" | custom-call | tf_op jit(solution)/shard_map/pallas_call | solution.py:400
  56.3 9.2 %shard_map.105 = (bf16[64,768]{1,0:T(8,128)(2,1)}, bf16[64,768]{1,0:T(8,128)(2,1)}) custom-call(bf16[128,768]{1,0:T(8,128)(2,1)} %get-tuple-element.16.ru, bf16[128,768]{1,0:T(8,128)(2,1)} %get-tuple-element.17.rv, bf16[64,768]{1,0:T(8,128)(2,1)} %x_ref.3, bf16[64,768]{1,0:T(8,128)(2,1)} %dy_ref.3, f32[72,128]{1,0:T(8,128)} %shard_map.102.g_ref), custom_call_target="tpu_custom_call" | custom-call | tf_op jit(solution)/shard_map/pallas_call | solution.py:415
  65.5 1.5 %copy.13 = bf16[64,768]{1,0:T(8,128)(2,1)} copy(bf16[64,768]{1,0:T(8,128)(2,1)} %get-tuple-element.26) | data formatting | bytes 196608
  67.0 1.5 %copy.14 = bf16[64,768]{1,0:T(8,128)(2,1)} copy(bf16[64,768]{1,0:T(8,128)(2,1)} %get-tuple-element.27) | data formatting | bytes 196608
